TPU v7x, 32 devices: a whole 2x2x4 slice. The times are simulated.
32 devices in a mesh: sky: 8 (over y, x, core), tm: 4 (over z).
Axes of the slice: x: 2, y: 2, z: 4, core: 2. Of those that a mesh axis runs over, the one named last changes fastest.
Arguments:
- obs_source: int32 [131072], P(('sky', 'tm')), may hold values from 0 to 1023
- obs_knot: int32 [131072], P(('sky', 'tm')), may hold values from 0 to 2047, as said below
- obs_count: int32 [32], P(('sky', 'tm')), may hold values from 256 to 4096, as said below
- src_design: float32 [5, 131072], P(None, ('sky', 'tm')), may hold values from -3 to 3
- att_design: float32 [4, 131072], P(None, ('sky', 'tm')), may hold values from -6 to 6
- obs_phase: float32 [131072], P(('sky', 'tm')), may hold values from 0 to 1
- obs_value: float32 [131072], P(('sky', 'tm')), may hold values from -6 to 6
- src_prior: float32 [5, 8192], P(None, 'sky'), may hold values from 1 to 16
Outputs:
- att_solution: float32 [4, 4, 2048], P(None, 'tm', 'sky')
- att_residual: float32 [4, 4, 2048], P(None, 'tm', 'sky')
- source_solution: float32 [5, 8192], P(None, 'sky')
Inputs may be any that keep to these rules, and one draw needn't show every extreme that they name: Block b holds the 4096 observation slots o with o // 4096 = b; with i = b // 4 its sources are the sources i * 1024 + obs_source. With j = b % 4 for the observation's block b, its four spline knots are j * 2048 + obs_knot and the next three. In every block, each range of 256 values r * 256 to r * 256 + 255 of obs_knot holds exactly 512 of the block's slots. `obs_count`: each count is 4096 divided by 1, 2, 4, 8 or 16; the live slots of a block are its first ones; some block is full.
All inputs are finite; a program needn't handle non-finite values.
Results may differ from a plain program's by a relative error of at most 0.0001.
Values sent between devices are 32-bit elements; how exact they have to be, the bound alone decides.
A program may use at most 64 MiB of HBM per device.

v0:
```python
import jax
import jax.numpy as jnp
from jax import lax
from jax.sharding import PartitionSpec as P

ITERS = 2
SRC_DEV = 1024
KN_DEV = 256
damping = 0.5
entry_pairs = [(row_at, col_at) for row_at in range(5) for col_at in range(row_at + 1)]


def shifted(value, axis, steps):
    count = lax.axis_size(axis)
    first, last = (max(0, -steps), min(count, count - steps))
    return lax.ppermute(value, axis, [(source, source + steps) for source in range(first, last)])


def spline_taps(phase):
    squared = phase * phase
    cubed = squared * phase
    rest = 1.0 - phase
    return (
        rest * rest * rest / 6.0,
        (3.0 * cubed - 6.0 * squared + 4.0) / 6.0,
        (-3.0 * cubed + 3.0 * squared + 3.0 * phase + 1.0) / 6.0,
        cubed / 6.0,
    )


def factorize(normal):
    factor = {}
    for row_at in range(5):
        for col_at in range(row_at + 1):
            running = normal[row_at, col_at]
            for inner_at in range(col_at):
                running = running - factor[row_at, inner_at] * factor[col_at, inner_at]
            if row_at == col_at:
                factor[row_at, row_at] = jnp.sqrt(running)
            else:
                factor[row_at, col_at] = running / factor[col_at, col_at]
    return factor


def chol_solve(factor, target):
    forward = []
    for row_at in range(5):
        running = target[row_at]
        for inner_at in range(row_at):
            running = running - factor[row_at, inner_at] * forward[inner_at]
        forward.append(running / factor[row_at, row_at])
    result = [None] * 5
    for row_at in reversed(range(5)):
        running = forward[row_at]
        for inner_at in range(row_at + 1, 5):
            running = running - factor[inner_at, row_at] * result[inner_at]
        result[row_at] = running / factor[row_at, row_at]
    return jnp.stack(result)


def source_total(source, rows, count):
    return jnp.zeros((rows.shape[0], count), jnp.float32).at[:, source].add(rows)


def knot_values(padded, knot, design, tap_weights):
    summed = jnp.zeros(knot.shape, jnp.float32)
    for tap_at in range(4):
        picked = jnp.take(padded, knot + tap_at, axis=1)
        summed = summed + tap_weights[tap_at] * jnp.sum(design * picked, axis=0)
    return summed


def knot_total(knot, design, tap_weights, weight_vec, extent):
    summed = jnp.zeros((design.shape[0], extent + 3), jnp.float32)
    for tap_at in range(4):
        summed = summed.at[:, knot + tap_at].add(design * (tap_weights[tap_at] * weight_vec))
    return summed


def eliminate(factor, source, design, values_obs, source_sums):
    solved = chol_solve(factor, [source_sums[row_at] for row_at in range(5)])
    fitted = jnp.sum(design * jnp.take(solved, source, axis=1), axis=0)
    return values_obs - fitted


def shards(
    obs_source, obs_knot, obs_count, src_design, att_design, obs_phase, obs_value, src_prior
):
    sky_count = lax.axis_size("sky")
    seg_knots = KN_DEV * sky_count
    slot_count = obs_source.shape[0]
    live_mask = (jnp.arange(slot_count, dtype=jnp.int32) < obs_count[0]).astype(jnp.float32)
    src_rows = src_design * live_mask
    att_rows = att_design * live_mask
    observed = obs_value * live_mask
    tap_weights = spline_taps(obs_phase)
    products = jnp.stack(
        [src_rows[row_at] * src_rows[col_at] for row_at, col_at in entry_pairs]
        + [src_rows[row_at] * observed for row_at in range(5)]
    )
    sums = lax.psum(source_total(obs_source, products, SRC_DEV), "tm")
    normal = {}
    for entry_at, pair in enumerate(entry_pairs):
        normal[pair] = sums[entry_at] + (src_prior[pair[0]] if pair[0] == pair[1] else 0.0)
    factor = factorize(normal)

    def source_part(values_obs):
        return lax.psum(source_total(obs_source, src_rows * values_obs, SRC_DEV), "tm")

    def along_knots(field):
        segment = lax.all_gather(field, "sky", axis=1, tiled=True)
        next_edge = shifted(segment[:, :3], "tm", -1)
        padded = jnp.concatenate([segment, next_edge], axis=1)
        return knot_values(padded, obs_knot, att_rows, tap_weights)

    def back_to_knots(cleaned):
        summed = knot_total(obs_knot, att_rows, tap_weights, cleaned, seg_knots)
        overflow = shifted(summed[:, seg_knots:], "tm", 1)
        partial_value = summed[:, :seg_knots].at[:, :3].add(overflow)
        return lax.psum_scatter(partial_value, "sky", scatter_dimension=1, tiled=True)

    def norm_sum(partial_value):
        return lax.psum(partial_value, ("sky", "tm"))

    cleaned = eliminate(factor, obs_source, src_rows, observed, sums[15:])
    residual = back_to_knots(cleaned)
    solution = jnp.zeros_like(residual)
    direction = residual
    norm_now = norm_sum(jnp.sum(residual * residual))
    for repeat in range(ITERS):
        image_obs = along_knots(direction)
        cleaned = eliminate(factor, obs_source, src_rows, image_obs, source_part(image_obs))
        mapped = back_to_knots(cleaned) + damping * direction
        alpha_step = norm_now / lax.psum(jnp.sum(direction * mapped), ("sky", "tm"))
        solution = solution + alpha_step * direction
        residual = residual - alpha_step * mapped
        norm_next = norm_sum(jnp.sum(residual * residual))
        direction = residual + norm_next / norm_now * direction
        norm_now = norm_next
    fitted = observed - along_knots(solution)
    source_solution = chol_solve(factor, [row for row in source_part(fitted)])
    return (solution[:, None, :], residual[:, None, :], source_solution)


def solution(mesh):
    placed = (
        P(("sky", "tm")),
        P(("sky", "tm")),
        P(("sky", "tm")),
        P(None, ("sky", "tm")),
        P(None, ("sky", "tm")),
        P(("sky", "tm")),
        P(("sky", "tm")),
        P(None, "sky"),
    )
    return jax.shard_map(
        shards,
        mesh=mesh,
        in_specs=placed,
        out_specs=(P(None, "tm", "sky"), P(None, "tm", "sky"), P(None, "sky")),
        check_vma=False,
    )
```

profile of v0, /device:TPU:0, one launch (start us, length us, event | category | flops | bytes accessed | tf_op | source)
XLA Modules:
  0.0 1068.1 jit_solution(9590675632088410657)
XLA Ops:
  11.7 22.5 %scatter_custom_fusion = f32[20,1024]{0,1:T(8,128)S(1)} fusion(s32[4096]{0:T(1024)S(1)} %get-tuple-element.173, f32[4096,20]{1,0:T(8,128)S(1)} %copy.271, f32[]{:T(128)} %constant.111.clone.1), kind=kCustom, calls=%fused_computation.113 | custom fusion | flops 81920 | bytes 81924 | tf_op jit(solution)/shard_map/scatter-add | solution.py:62
  37.1 35.3 %all-reduce.3.cloned.1.call-done = f32[20,1024]{1,0:T(8,128)} async-done(((f32[20,1024]{1,0:T(8,128)}), f32[20,1024]{1,0:T(8,128)}) %all-reduce.3.cloned.1.call-update) | async-done | bytes 81936 | tf_op jit(solution)/shard_map/psum | solution.py:101
  75.5 14.1 %gather_fusion = f32[4096,5]{1,0:T(8,128)} fusion(f32[5,1024]{0,1:T(8,128)S(1)} %copy.273, s32[4096]{0:T(1024)S(1)} %get-tuple-element.172), kind=kCustom, calls=%fused_computation.clone | custom fusion | bytes 180224 | tf_op jit(solution)/shard_map/jit(_take)/gather | solution.py:82
  92.0 25.3 %scatter_custom_fusion.1 = f32[4,2051]{0,1:T(8,128)S(1)} fusion(s32[4096]{0:T(1024)} %get-tuple-element.168, f32[4096]{0:T(1024)S(1)} %get-tuple-element.159, f32[]{:T(128)} %constant.111.clone.1, f32[4,4096]{0,1:T(8,128)S(1)} %copy.270, f32[4096]{0:T(1024)S(1)} %fusion.83), kind=kCustom, calls=%fused_computation.77 | custom fusion | flops 49152 | bytes 131632 | tf_op jit(solution)/shard_map/scatter-add | solution.py:76
  117.3 25.4 %scatter_custom_fusion.2 = f32[4,2051]{0,1:T(8,128)S(1)} fusion(f32[4,2051]{0,1:T(8,128)S(1)} %scatter_custom_fusion.1, s32[4096]{0:T(1024)} %get-tuple-element.166, f32[4096]{0:T(1024)S(1)} %get-tuple-element.158, f32[4,4096]{0,1:T(8,128)S(1)} %copy.270, f32[4096]{0:T(1024)S(1)} %fusion.83), kind=kCustom, calls=%fused_computation.75 | custom fusion | flops 49152 | bytes 2162736 | tf_op jit(solution)/shard_map/scatter-add | solution.py:76
  142.6 25.4 %scatter_custom_fusion.3 = f32[4,2051]{0,1:T(8,128)S(1)} fusion(f32[4,2051]{0,1:T(8,128)S(1)} %scatter_custom_fusion.2, s32[4096]{0:T(1024)} %get-tuple-element.167, f32[4096]{0:T(1024)S(1)} %get-tuple-element.157, f32[4,4096]{0,1:T(8,128)S(1)} %copy.270, f32[4096]{0:T(1024)S(1)} %fusion.83), kind=kCustom, calls=%fused_computation.73 | custom fusion | flops 49152 | bytes 2162736 | tf_op jit(solution)/shard_map/scatter-add | solution.py:76
  168.1 25.4 %scatter_custom_fusion.4 = f32[4,2051]{0,1:T(8,128)S(1)} fusion(f32[4,2051]{0,1:T(8,128)S(1)} %scatter_custom_fusion.3, s32[4096]{0:T(1024)S(1)} %get-tuple-element.171, f32[4096]{0:T(1024)S(1)} %get-tuple-element.106, f32[4,4096]{0,1:T(8,128)S(1)} %copy.270, f32[4096]{0:T(1024)S(1)} %fusion.83), kind=kCustom, calls=%fused_computation.71 | custom fusion | flops 49152 | bytes 2162736 | tf_op jit(solution)/shard_map/scatter-add | solution.py:76
  201.3 36.5 %reduce-scatter.10.cloned.1.call-done = f32[256,4]{1,0:T(8,128)} async-done(((f32[2048,4]{1,0:T(8,128)}), f32[256,4]{1,0:T(8,128)}) %reduce-scatter.10.cloned.1.call-update) | async-done | bytes 4112
  237.9 10.9 %all_gather.9 = f32[4,2048]{0,1:T(8,128)S(1)} all-gather(f32[4,256]{0,1:T(8,128)} %bitcast.131), channel_id=1, replica_groups=mesh['sky'=8,'tm'=4] {'sky'}, dimensions={1}, use_global_device_ids=true | all-gather | bytes 36864 | tf_op jit(solution)/shard_map/all_gather | solution.py:111
  250.1 4.2 collective-permute-done.1
  254.3 14.1 %gather_fusion.4 = f32[4096,4]{1,0:T(8,128)} fusion(f32[4,2051]{0,1:T(8,128)S(1)} %constant_dynamic-update-slice_fusion, s32[4096]{0:T(1024)S(1)} %get-tuple-element.164), kind=kCustom, calls=%fused_computation.6.clone | custom fusion | bytes 147456 | tf_op jit(solution)/shard_map/jit(_take)/gather | solution.py:68
  268.4 14.1 %gather_fusion.3 = f32[4096,4]{1,0:T(8,128)} fusion(f32[4,2051]{0,1:T(8,128)S(1)} %constant_dynamic-update-slice_fusion, s32[4096]{0:T(1024)S(1)} %get-tuple-element.169), kind=kCustom, calls=%fused_computation.5.clone | custom fusion | bytes 147456 | tf_op jit(solution)/shard_map/jit(_take)/gather | solution.py:68
  282.5 14.1 %gather_fusion.2 = f32[4096,4]{1,0:T(8,128)} fusion(f32[4,2051]{0,1:T(8,128)S(1)} %constant_dynamic-update-slice_fusion, s32[4096]{0:T(1024)S(1)} %get-tuple-element.170), kind=kCustom, calls=%fused_computation.4.clone | custom fusion | bytes 147456 | tf_op jit(solution)/shard_map/jit(_take)/gather | solution.py:68
  296.5 14.1 %gather_fusion.1 = f32[4096,4]{1,0:T(8,128)} fusion(f32[4,2051]{0,1:T(8,128)S(1)} %constant_dynamic-update-slice_fusion, s32[4096]{0:T(1024)S(1)} %get-tuple-element.165), kind=kCustom, calls=%fused_computation.1.clone | custom fusion | bytes 147456 | tf_op jit(solution)/shard_map/jit(_take)/gather | solution.py:68
  310.6 8.9 fusion.27
  321.7 22.8 %scatter_custom_fusion.5 = f32[5,1024]{0,1:T(8,128)S(1)} fusion(s32[4096]{0:T(1024)} %copy-done.35, f32[4096,5]{1,0:T(8,128)} %copy.277, f32[]{:T(128)} %constant.111.clone.1), kind=kCustom, calls=%fused_computation.111 | custom fusion | flops 20480 | bytes 20992 | tf_op jit(solution)/shard_map/scatter-add | solution.py:62
  344.6 17.2 %psum.58 = f32[5,1024]{1,0:T(8,128)S(1)} all-reduce(f32[5,1024]{1,0:T(8,128)S(1)} %copy.278), channel_id=1, replica_groups=mesh['sky'=8,'tm'=4] {'tm'}, use_global_device_ids=true, to_apply=%region_16.19 | all-reduce | flops 5120 | bytes 40960 | tf_op jit(solution)/shard_map/psum | solution.py:108
  363.1 14.1 %gather_fusion.5 = f32[4096,5]{1,0:T(8,128)} fusion(f32[5,1024]{0,1:T(8,128)S(1)} %copy.279, s32[4096]{0:T(1024)S(1)} %get-tuple-element.172), kind=kCustom, calls=%fused_computation.2.clone | custom fusion | bytes 180224 | tf_op jit(solution)/shard_map/jit(_take)/gather | solution.py:82
  379.6 25.3 %scatter_custom_fusion.6 = f32[4,2051]{0,1:T(8,128)S(1)} fusion(s32[4096]{0:T(1024)} %get-tuple-element.168, f32[4096]{0:T(1024)S(1)} %get-tuple-element.156, f32[]{:T(128)} %constant.111.clone.1, f32[4,4096]{0,1:T(8,128)S(1)} %copy.270, f32[4096]{0:T(1024)S(1)} %fusion.83), kind=kCustom, calls=%fused_computation.61 | custom fusion | flops 49152 | bytes 131632 | tf_op jit(solution)/shard_map/scatter-add | solution.py:76
  404.8 25.6 %scatter_custom_fusion.7 = f32[4,2051]{0,1:T(8,128)S(1)} fusion(f32[4,2051]{0,1:T(8,128)S(1)} %scatter_custom_fusion.6, s32[4096]{0:T(1024)} %get-tuple-element.166, f32[4096]{0:T(1024)S(1)} %get-tuple-element.155, f32[4,4096]{0,1:T(8,128)S(1)} %copy.270, f32[4096]{0:T(1024)S(1)} %fusion.83), kind=kCustom, calls=%fused_computation.59 | custom fusion | flops 49152 | bytes 2162736 | tf_op jit(solution)/shard_map/scatter-add | solution.py:76
  430.5 25.4 %scatter_custom_fusion.8 = f32[4,2051]{0,1:T(8,128)S(1)} fusion(f32[4,2051]{0,1:T(8,128)S(1)} %scatter_custom_fusion.7, s32[4096]{0:T(1024)} %get-tuple-element.167, f32[4096]{0:T(1024)S(1)} %get-tuple-element.154, f32[4,4096]{0,1:T(8,128)S(1)} %copy.270, f32[4096]{0:T(1024)S(1)} %fusion.83), kind=kCustom, calls=%fused_computation.57 | custom fusion | flops 49152 | bytes 2162736 | tf_op jit(solution)/shard_map/scatter-add | solution.py:76
  455.8 25.4 %scatter_custom_fusion.9 = f32[4,2051]{0,1:T(8,128)S(1)} fusion(f32[4,2051]{0,1:T(8,128)S(1)} %scatter_custom_fusion.8, s32[4096]{0:T(1024)} %copy-done.36, f32[4096]{0:T(1024)S(1)} %get-tuple-element.95, f32[4,4096]{0,1:T(8,128)S(1)} %copy.270, f32[4096]{0:T(1024)S(1)} %fusion.83), kind=kCustom, calls=%fused_computation.55 | custom fusion | flops 49152 | bytes 2162736 | tf_op jit(solution)/shard_map/scatter-add | solution.py:76
  487.6 36.2 %reduce-scatter.12.cloned.1.call-done = f32[256,4]{1,0:T(8,128)} async-done(((f32[2048,4]{1,0:T(8,128)}), f32[256,4]{1,0:T(8,128)}) %reduce-scatter.12.cloned.1.call-update) | async-done | bytes 4112
  525.4 39.5 %all-reduce = (f32[]{:T(128)}, f32[]{:T(128)}) all-reduce(f32[]{:T(128)} %get-tuple-element.72, f32[]{:T(128)} %get-tuple-element.71), channel_id=1, replica_groups=mesh['sky'=8,'tm'=4] {'sky','tm'}, use_global_device_ids=true, to_apply=%region_10.12 | all-reduce | flops 2 | bytes 16 | tf_op jit(solution)/shard_map/psum | solution.py:123
  566.7 41.3 %psum.60 = f32[]{:T(128)} all-reduce(f32[]{:T(128)} %multiply_reduce_fusion.1), channel_id=1, replica_groups=mesh['sky'=8,'tm'=4] {'sky','tm'}, use_global_device_ids=true, to_apply=%region_26.29 | all-reduce | flops 1 | bytes 8 | tf_op jit(solution)/shard_map/psum | solution.py:123
  609.2 10.1 all_gather.10
  625.2 14.1 %gather_fusion.9 = f32[4096,4]{1,0:T(8,128)} fusion(f32[4,2051]{0,1:T(8,128)S(1)} %copy.282, s32[4096]{0:T(1024)S(1)} %get-tuple-element.164), kind=kCustom, calls=%fused_computation.10.clone | custom fusion | bytes 147456 | tf_op jit(solution)/shard_map/jit(_take)/gather | solution.py:68
  639.2 14.1 %gather_fusion.8 = f32[4096,4]{1,0:T(8,128)} fusion(f32[4,2051]{0,1:T(8,128)S(1)} %copy.282, s32[4096]{0:T(1024)S(1)} %get-tuple-element.169), kind=kCustom, calls=%fused_computation.9.clone | custom fusion | bytes 147456 | tf_op jit(solution)/shard_map/jit(_take)/gather | solution.py:68
  653.3 14.1 %gather_fusion.7 = f32[4096,4]{1,0:T(8,128)} fusion(f32[4,2051]{0,1:T(8,128)S(1)} %copy.282, s32[4096]{0:T(1024)S(1)} %get-tuple-element.170), kind=kCustom, calls=%fused_computation.8.clone | custom fusion | bytes 147456 | tf_op jit(solution)/shard_map/jit(_take)/gather | solution.py:68
  667.4 14.1 %gather_fusion.6 = f32[4096,4]{1,0:T(8,128)} fusion(f32[4,2051]{0,1:T(8,128)S(1)} %copy.282, s32[4096]{0:T(1024)S(1)} %get-tuple-element.165), kind=kCustom, calls=%fused_computation.7.clone | custom fusion | bytes 147456 | tf_op jit(solution)/shard_map/jit(_take)/gather | solution.py:68
  681.5 9.5 fusion.15
  693.1 22.8 %scatter_custom_fusion.10 = f32[5,1024]{0,1:T(8,128)S(1)} fusion(s32[4096]{0:T(1024)} %copy-done.35, f32[4096,5]{1,0:T(8,128)} %copy.286, f32[]{:T(128)} %constant.111.clone.1), kind=kCustom, calls=%fused_computation.109 | custom fusion | flops 20480 | bytes 20992 | tf_op jit(solution)/shard_map/scatter-add | solution.py:62
  716.1 16.2 %psum.61 = f32[5,1024]{1,0:T(8,128)S(1)} all-reduce(f32[5,1024]{1,0:T(8,128)S(1)} %copy.287), channel_id=1, replica_groups=mesh['sky'=8,'tm'=4] {'tm'}, use_global_device_ids=true, to_apply=%region_32.35 | all-reduce | flops 5120 | bytes 40960 | tf_op jit(solution)/shard_map/psum | solution.py:108
  733.6 14.1 %gather_fusion.10 = f32[4096,5]{1,0:T(8,128)} fusion(f32[5,1024]{0,1:T(8,128)S(1)} %copy.288, s32[4096]{0:T(1024)S(1)} %get-tuple-element.172), kind=kCustom, calls=%fused_computation.3.clone | custom fusion | bytes 180224 | tf_op jit(solution)/shard_map/jit(_take)/gather | solution.py:82
  750.0 25.3 %scatter_custom_fusion.11 = f32[4,2051]{0,1:T(8,128)S(1)} fusion(s32[4096]{0:T(1024)} %get-tuple-element.168, f32[4096]{0:T(1024)S(1)} %get-tuple-element.153, f32[]{:T(128)} %constant.111.clone.1, f32[4,4096]{0,1:T(8,128)S(1)} %copy.270, f32[4096]{0:T(1024)S(1)} %fusion.83), kind=kCustom, calls=%fused_computation.45 | custom fusion | flops 49152 | bytes 131632 | tf_op jit(solution)/shard_map/scatter-add | solution.py:76
  775.3 25.4 %scatter_custom_fusion.12 = f32[4,2051]{0,1:T(8,128)S(1)} fusion(f32[4,2051]{0,1:T(8,128)S(1)} %scatter_custom_fusion.11, s32[4096]{0:T(1024)} %get-tuple-element.166, f32[4096]{0:T(1024)S(1)} %get-tuple-element.152, f32[4,4096]{0,1:T(8,128)S(1)} %copy.270, f32[4096]{0:T(1024)S(1)} %fusion.83), kind=kCustom, calls=%fused_computation.43 | custom fusion | flops 49152 | bytes 2162736 | tf_op jit(solution)/shard_map/scatter-add | solution.py:76
  800.7 25.4 %scatter_custom_fusion.13 = f32[4,2051]{0,1:T(8,128)S(1)} fusion(f32[4,2051]{0,1:T(8,128)S(1)} %scatter_custom_fusion.12, s32[4096]{0:T(1024)} %get-tuple-element.167, f32[4096]{0:T(1024)S(1)} %get-tuple-element.151, f32[4,4096]{0,1:T(8,128)S(1)} %copy.270, f32[4096]{0:T(1024)S(1)} %fusion.83), kind=kCustom, calls=%fused_computation.41 | custom fusion | flops 49152 | bytes 2162736 | tf_op jit(solution)/shard_map/scatter-add | solution.py:76
  826.1 25.6 %scatter_custom_fusion.14 = f32[4,2051]{0,1:T(8,128)S(1)} fusion(f32[4,2051]{0,1:T(8,128)S(1)} %scatter_custom_fusion.13, s32[4096]{0:T(1024)} %copy-done.36, f32[4096]{0:T(1024)S(1)} %get-tuple-element.84, f32[4,4096]{0,1:T(8,128)S(1)} %copy.270, f32[4096]{0:T(1024)S(1)} %fusion.83), kind=kCustom, calls=%fused_computation.39 | custom fusion | flops 49152 | bytes 2162736 | tf_op jit(solution)/shard_map/scatter-add | solution.py:76
  857.5 36.8 %reduce-scatter.14.cloned.1.call-done = f32[256,4]{1,0:T(8,128)} async-done(((f32[2048,4]{1,0:T(8,128)}), f32[256,4]{1,0:T(8,128)}) %reduce-scatter.14.cloned.1.call-update) | async-done | bytes 4112
  896.0 39.4 %psum.62 = f32[]{:T(128)} all-reduce(f32[]{:T(128)} %multiply_reduce_fusion), channel_id=1, replica_groups=mesh['sky'=8,'tm'=4] {'sky','tm'}, use_global_device_ids=true, to_apply=%region_40.43 | all-reduce | flops 1 | bytes 8 | tf_op jit(solution)/shard_map/psum | solution.py:134
  937.3 10.1 all_gather.11
  953.8 14.1 %gather_fusion.14 = f32[4096,4]{1,0:T(8,128)} fusion(f32[4,2051]{0,1:T(8,128)S(1)} %copy.291, s32[4096]{0:T(1024)S(1)} %get-tuple-element.164), kind=kCustom, calls=%fused_computation.14.clone | custom fusion | bytes 147456 | tf_op jit(solution)/shard_map/jit(_take)/gather | solution.py:68
  967.9 14.1 %gather_fusion.13 = f32[4096,4]{1,0:T(8,128)} fusion(f32[4,2051]{0,1:T(8,128)S(1)} %copy.291, s32[4096]{0:T(1024)S(1)} %get-tuple-element.169), kind=kCustom, calls=%fused_computation.13.clone | custom fusion | bytes 147456 | tf_op jit(solution)/shard_map/jit(_take)/gather | solution.py:68
  982.0 14.1 %gather_fusion.12 = f32[4096,4]{1,0:T(8,128)} fusion(f32[4,2051]{0,1:T(8,128)S(1)} %copy.291, s32[4096]{0:T(1024)S(1)} %get-tuple-element.170), kind=kCustom, calls=%fused_computation.12.clone | custom fusion | bytes 147456 | tf_op jit(solution)/shard_map/jit(_take)/gather | solution.py:68
  996.0 14.1 %gather_fusion.11 = f32[4096,4]{1,0:T(8,128)} fusion(f32[4,2051]{0,1:T(8,128)S(1)} %copy.291, s32[4096]{0:T(1024)S(1)} %get-tuple-element.165), kind=kCustom, calls=%fused_computation.11.clone | custom fusion | bytes 147456 | tf_op jit(solution)/shard_map/jit(_take)/gather | solution.py:68
  1010.2 8.9 fusion.3
  1019.8 22.6 %scatter_custom_fusion.15 = f32[5,1024]{0,1:T(8,128)S(1)} fusion(s32[4096]{0:T(1024)} %copy-done.35, f32[4096,5]{1,0:T(8,128)S(1)} %copy.295, f32[]{:T(128)} %constant.111.clone.1), kind=kCustom, calls=%fused_computation.107 | custom fusion | flops 20480 | bytes 20992 | tf_op jit(solution)/shard_map/scatter-add | solution.py:62
  1042.6 17.2 %psum.63 = f32[5,1024]{1,0:T(8,128)S(1)} all-reduce(f32[5,1024]{1,0:T(8,128)S(1)} %copy.296), channel_id=1, replica_groups=mesh['sky'=8,'tm'=4] {'tm'}, use_global_device_ids=true, to_apply=%region_46.49 | all-reduce | flops 5120 | bytes 40960 | tf_op jit(solution)/shard_map/psum | solution.py:108
  (177 shorter events, 64.0 us)
Async XLA Ops:
  7.2 65.2 %all-reduce.3.cloned.1.call-start = ((), (), s32[]{:S(2)}) async-start(), calls=%async_computation.3 | async-start | bytes 196608 | tf_op jit(solution)/shard_map/psum | solution.py:101
  9.8 25.2 %copy-start.35 = (s32[4096]{0:T(1024)}, s32[4096]{0:T(1024)S(1)}, u32[]{:S(2)}) copy-start(s32[4096]{0:T(1024)S(1)} %get-tuple-element.173) | copy-start | bytes 49156
  10.5 24.6 %copy-start.25 = (s32[4096]{0:T(1024)S(1)}, s32[4096]{0:T(1024)}, u32[]{:S(2)}) copy-start(s32[4096]{0:T(1024)} %param.19) | copy-start | bytes 49156
  11.0 24.7 %copy-start.24 = (s32[4096]{0:T(1024)S(1)}, s32[4096]{0:T(1024)}, u32[]{:S(2)}) copy-start(s32[4096]{0:T(1024)} %param.18) | copy-start | bytes 49156
  11.0 24.7 %copy-start.23 = (f32[4,4096]{1,0:T(4,128)S(1)}, f32[4,4096]{1,0:T(4,128)}, u32[]{:S(2)}) copy-start(f32[4,4096]{1,0:T(4,128)} %param.22) | copy-start | bytes 196612
  11.7 60.7 %copy-start.34 = (f32[5,1024]{1,0:T(8,128)S(1)}, f32[5,1024]{1,0:T(8,128)}, u32[]{:S(2)}) copy-start(f32[5,1024]{1,0:T(8,128)} %param.25) | copy-start | bytes 61444
  35.0 202.8 %reduce-scatter.10.cloned.1.call-start = ((), (), s32[]{:S(2)}) async-start(), calls=%async_computation.4 | async-start | bytes 1179648
  35.7 132.3 %copy-start.36 = (s32[4096]{0:T(1024)}, s32[4096]{0:T(1024)S(1)}, u32[]{:S(2)}) copy-start(s32[4096]{0:T(1024)S(1)} %get-tuple-element.171) | copy-start | bytes 49156
  35.7 343.7 %copy-start.21 = (pred[4096]{0:T(1024)(128)(4,1)}, pred[4096]{0:T(1024)(128)(4,1)S(1)}, u32[]{:S(2)}) copy-start(pred[4096]{0:T(1024)(128)(4,1)S(1)} %compare_and_fusion.4) | copy-start | bytes 12292
  73.6 288.4 %copy-start.3 = (f32[1,1024]{1,0:T(1,128)}, f32[1,1024]{1,0:T(1,128)S(1)}, u32[]{:S(2)}) copy-start(f32[1,1024]{1,0:T(1,128)S(1)} %get-tuple-element.128) | copy-start | bytes 12292
  73.6 288.4 %copy-start.5 = (f32[1,1024]{1,0:T(1,128)}, f32[1,1024]{1,0:T(1,128)S(1)}, u32[]{:S(2)}) copy-start(f32[1,1024]{1,0:T(1,128)S(1)} %get-tuple-element.129) | copy-start | bytes 12292
  73.6 288.4 %copy-start.7 = (f32[1,1024]{1,0:T(1,128)}, f32[1,1024]{1,0:T(1,128)S(1)}, u32[]{:S(2)}) copy-start(f32[1,1024]{1,0:T(1,128)S(1)} %get-tuple-element.130) | copy-start | bytes 12292
  73.6 18.2 %copy-start = (f32[5,4096]{1,0:T(8,128)S(1)}, f32[5,4096]{1,0:T(8,128)}, u32[]{:S(2)}) copy-start(f32[5,4096]{1,0:T(8,128)} %param.21) | copy-start | bytes 245764
  75.3 16.6 %copy-start.1 = (f32[4096]{0:T(1024)S(1)}, f32[4096]{0:T(1024)}, u32[]{:S(2)}) copy-start(f32[4096]{0:T(1024)} %param.23) | copy-start | bytes 49156
  75.3 16.6 %copy-start.9 = (f32[4096]{0:T(1024)S(1)}, f32[4096]{0:T(1024)}, u32[]{:S(2)}) copy-start(f32[4096]{0:T(1024)} %param.24) | copy-start | bytes 49156
  194.6 4.6 collective-permute-start
  201.2 322.6 %reduce-scatter.12.cloned.1.call-start = ((), (), s32[]{:S(2)}) async-start(), calls=%async_computation.5 | async-start | bytes 1179648
  201.3 109.3 %copy-start.13 = (pred[4096]{0:T(1024)(128)(4,1)}, pred[4096]{0:T(1024)(128)(4,1)S(1)}, u32[]{:S(2)}) copy-start(pred[4096]{0:T(1024)(128)(4,1)S(1)} %get-tuple-element.160) | copy-start | bytes 12292
  201.3 109.3 %copy-start.15 = (pred[4096]{0:T(1024)(128)(4,1)}, pred[4096]{0:T(1024)(128)(4,1)S(1)}, u32[]{:S(2)}) copy-start(pred[4096]{0:T(1024)(128)(4,1)S(1)} %get-tuple-element.161) | copy-start | bytes 12292
  201.3 109.3 %copy-start.17 = (pred[4096]{0:T(1024)(128)(4,1)}, pred[4096]{0:T(1024)(128)(4,1)S(1)}, u32[]{:S(2)}) copy-start(pred[4096]{0:T(1024)(128)(4,1)S(1)} %get-tuple-element.162) | copy-start | bytes 12292
  201.3 109.3 %copy-start.19 = (pred[4096]{0:T(1024)(128)(4,1)}, pred[4096]{0:T(1024)(128)(4,1)S(1)}, u32[]{:S(2)}) copy-start(pred[4096]{0:T(1024)(128)(4,1)S(1)} %get-tuple-element.163) | copy-start | bytes 12292
  248.8 5.5 collective-permute-start.1
  319.6 42.4 %copy-start.26 = (f32[1,1024]{1,0:T(1,128)S(1)}, f32[1,1024]{1,0:T(1,128)}, u32[]{:S(2)}) copy-start(f32[1,1024]{1,0:T(1,128)} %get-tuple-element.113) | copy-start | bytes 12292
  319.6 42.4 %copy-start.28 = (f32[1,1024]{1,0:T(1,128)S(1)}, f32[1,1024]{1,0:T(1,128)}, u32[]{:S(2)}) copy-start(f32[1,1024]{1,0:T(1,128)} %get-tuple-element.114) | copy-start | bytes 12292
  319.6 42.4 %copy-start.30 = (f32[1,1024]{1,0:T(1,128)S(1)}, f32[1,1024]{1,0:T(1,128)}, u32[]{:S(2)}) copy-start(f32[1,1024]{1,0:T(1,128)} %get-tuple-element.115) | copy-start | bytes 12292
  319.6 42.4 %copy-start.32 = (f32[1,1024]{1,0:T(1,128)S(1)}, f32[1,1024]{1,0:T(1,128)}, u32[]{:S(2)}) copy-start(f32[1,1024]{1,0:T(1,128)} %get-tuple-element.116) | copy-start | bytes 12292
  481.2 6.3 copy-start.2
  482.3 2.6 collective-permute-start.2
  487.5 406.9 %reduce-scatter.14.cloned.1.call-start = ((), (), s32[]{:S(2)}) async-start(), calls=%async_computation.6 | async-start | bytes 1179648
  487.6 137.1 %copy-start.11 = (f32[4,256]{1,0:T(4,128)}, f32[4,256]{1,0:T(4,128)S(1)}, u32[]{:S(2)}) copy-start(f32[4,256]{1,0:T(4,128)S(1)} %copy.300) | copy-start | bytes 12292
  619.3 5.5 collective-permute-start.3
  691.0 41.3 %copy-start.4 = (f32[1,1024]{1,0:T(1,128)S(1)}, f32[1,1024]{1,0:T(1,128)}, u32[]{:S(2)}) copy-start(f32[1,1024]{1,0:T(1,128)} %copy-done.3) | copy-start | bytes 12292
  691.0 41.3 %copy-start.6 = (f32[1,1024]{1,0:T(1,128)S(1)}, f32[1,1024]{1,0:T(1,128)}, u32[]{:S(2)}) copy-start(f32[1,1024]{1,0:T(1,128)} %copy-done.5) | copy-start | bytes 12292
  691.0 41.3 %copy-start.8 = (f32[1,1024]{1,0:T(1,128)S(1)}, f32[1,1024]{1,0:T(1,128)}, u32[]{:S(2)}) copy-start(f32[1,1024]{1,0:T(1,128)} %copy-done.7) | copy-start | bytes 12292
  691.0 41.4 %copy-start.27 = (f32[1,1024]{1,0:T(1,128)S(1)}, f32[1,1024]{1,0:T(1,128)}, u32[]{:S(2)}) copy-start(f32[1,1024]{1,0:T(1,128)} %get-tuple-element.113) | copy-start | bytes 12292
  691.0 41.4 %copy-start.29 = (f32[1,1024]{1,0:T(1,128)S(1)}, f32[1,1024]{1,0:T(1,128)}, u32[]{:S(2)}) copy-start(f32[1,1024]{1,0:T(1,128)} %get-tuple-element.114) | copy-start | bytes 12292
  691.0 41.4 %copy-start.31 = (f32[1,1024]{1,0:T(1,128)S(1)}, f32[1,1024]{1,0:T(1,128)}, u32[]{:S(2)}) copy-start(f32[1,1024]{1,0:T(1,128)} %get-tuple-element.115) | copy-start | bytes 12292
  691.0 41.4 %copy-start.33 = (f32[1,1024]{1,0:T(1,128)S(1)}, f32[1,1024]{1,0:T(1,128)}, u32[]{:S(2)}) copy-start(f32[1,1024]{1,0:T(1,128)} %get-tuple-element.116) | copy-start | bytes 12292
  732.4 17.5 %copy-start.22 = (pred[4096]{0:T(1024)(128)(4,1)S(1)}, pred[4096]{0:T(1024)(128)(4,1)}, u32[]{:S(2)}) copy-start(pred[4096]{0:T(1024)(128)(4,1)} %copy-done.21) | copy-start | bytes 12292
  851.6 85.0 %copy-start.12 = (f32[4,256]{1,0:T(4,128)S(1)}, f32[4,256]{1,0:T(4,128)}, u32[]{:S(2)}) copy-start(f32[4,256]{1,0:T(4,128)} %copy-done.11) | copy-start | bytes 12292
  852.7 2.8 collective-permute-start.4
  857.5 152.6 %copy-start.14 = (pred[4096]{0:T(1024)(128)(4,1)S(1)}, pred[4096]{0:T(1024)(128)(4,1)}, u32[]{:S(2)}) copy-start(pred[4096]{0:T(1024)(128)(4,1)} %copy-done.13) | copy-start | bytes 12292
  857.5 152.6 %copy-start.16 = (pred[4096]{0:T(1024)(128)(4,1)S(1)}, pred[4096]{0:T(1024)(128)(4,1)}, u32[]{:S(2)}) copy-start(pred[4096]{0:T(1024)(128)(4,1)} %copy-done.15) | copy-start | bytes 12292
  857.5 152.6 %copy-start.18 = (pred[4096]{0:T(1024)(128)(4,1)S(1)}, pred[4096]{0:T(1024)(128)(4,1)}, u32[]{:S(2)}) copy-start(pred[4096]{0:T(1024)(128)(4,1)} %copy-done.17) | copy-start | bytes 12292
  857.5 152.6 %copy-start.20 = (pred[4096]{0:T(1024)(128)(4,1)S(1)}, pred[4096]{0:T(1024)(128)(4,1)}, u32[]{:S(2)}) copy-start(pred[4096]{0:T(1024)(128)(4,1)} %copy-done.19) | copy-start | bytes 12292
  948.0 5.5 collective-permute-start.5
  1010.1 9.0 copy-start.10
Sparse Core Ops, SparseCore 0:
  35.1 37.1 all-reduce.2
  201.3 36.4 reduce-scatter.9
  487.6 36.1 reduce-scatter.11
  857.6 36.7 reduce-scatter.13
where the time goes:
time: 1080 us; the launch traced here: 1070 us
  other arithmetic  437 us (40%)
  local copies, waits for them, and re-layouts  238 us (22%)
  blocking collectives  202 us (19%)
  waiting for transfers between devices  161 us (15%)
  between operations  19.3 us (2%)
    scatter-add x12, other arithmetic, knot_total(): summed.at[:, knot + tap_at].add(design * (tap_weights[tap_at] * weight_vec))  305 us
    gather x12, local copies, waits for them, and re-layouts, knot_values(): picked = jnp.take(padded, knot + tap_at, axis=1)  169 us
    unnamed x7, waiting for transfers between devices  110 us
    scatter-add x4, other arithmetic, source_total(): jnp.zeros((rows.shape[0], count), jnp.float32).at[:, source].add(rows)  90.6 us
    psum x2, blocking collectives, norm_sum(): return lax.psum(partial_value, ('sky', 'tm'))  80.7 us
    psum x3, blocking collectives, source_part(): lax.psum(source_total(obs_source, src_rows * values_obs, SRC_DEV), 'tm')  50.7 us
    gather x6, local copies, waits for them, and re-layouts, eliminate(): fitted = jnp.sum(design * jnp.take(solved, source, axis=1), axis=0)  48.9 us
    psum x1, blocking collectives, shards(): alpha_step = norm_now / lax.psum(jnp.sum(direction * mapped), ('sky', 'tm'))  39.4 us
  transfers between devices with their start and end apart: 10, of which 10 were waited for; matrix products, arithmetic and copies ran while one was open for 0% of the time, Pallas kernels for 0%

commit v1 on v0

--- a/solution.py
+++ b/solution.py
@@ -120,7 +120,7 @@
         return lax.psum_scatter(partial_value, "sky", scatter_dimension=1, tiled=True)
 
     def norm_sum(partial_value):
-        return lax.psum(partial_value, ("sky", "tm"))
+        return jax.lax.psum(jax.lax.psum(partial_value, "sky"), "tm")
 
     cleaned = eliminate(factor, obs_source, src_rows, observed, sums[15:])
     residual = back_to_knots(cleaned)

time: 1080 us -> 1080 us (level)
    psum x1 -> x2, blocking collectives: 39.4 us -> 76.4 us  [shards(): alpha_step = norm_now / lax.psum(jnp.sum(direction * mapped), ('sky', 'tm'))]
    psum x2 -> x4, blocking collectives: 80.7 us -> 50.6 us  [norm_sum(): return jax.lax.psum(jax.lax.psum(partial_value, 'sky'), 'tm')]
where the time goes in v1:
time: 1080 us; the launch traced here: 1070 us
  other arithmetic  437 us (40%)
  local copies, waits for them, and re-layouts  238 us (22%)
  blocking collectives  207 us (19%)
  waiting for transfers between devices  161 us (15%)
  between operations  19.5 us (2%)
  starting transfers between devices  10.9 us (1%)
    scatter-add x12, other arithmetic, knot_total(): summed.at[:, knot + tap_at].add(design * (tap_weights[tap_at] * weight_vec))  305 us
    gather x12, local copies, waits for them, and re-layouts, knot_values(): picked = jnp.take(padded, knot + tap_at, axis=1)  169 us
    unnamed x7, waiting for transfers between devices  110 us
    scatter-add x4, other arithmetic, source_total(): jnp.zeros((rows.shape[0], count), jnp.float32).at[:, source].add(rows)  90.6 us
    psum x2, blocking collectives, shards(): alpha_step = norm_now / lax.psum(jnp.sum(direction * mapped), ('sky', 'tm'))  76.4 us
    psum x4, blocking collectives, norm_sum(): return jax.lax.psum(jax.lax.psum(partial_value, 'sky'), 'tm')  50.6 us
    psum x3, blocking collectives, source_part(): lax.psum(source_total(obs_source, src_rows * values_obs, SRC_DEV), 'tm')  50.2 us
    gather x6, local copies, waits for them, and re-layouts, eliminate(): fitted = jnp.sum(design * jnp.take(solved, source, axis=1), axis=0)  48.9 us
  transfers between devices with their start and end apart: 10, of which 10 were waited for; matrix products, arithmetic and copies ran while one was open for 0% of the time, Pallas kernels for 0%

profile of v1, /device:TPU:0, one launch (start us, length us, event | category | flops | bytes accessed | tf_op | source)
XLA Modules:
  0.0 1074.0 jit_solution(11422513508396761795)
XLA Ops:
  11.7 22.5 %scatter_custom_fusion = f32[20,1024]{0,1:T(8,128)S(1)} fusion(s32[4096]{0:T(1024)S(1)} %get-tuple-element.171, f32[4096,20]{1,0:T(8,128)S(1)} %copy.271, f32[]{:T(128)} %constant.111.clone.1), kind=kCustom, calls=%fused_computation.113 | custom fusion | flops 81920 | bytes 81924 | tf_op jit(solution)/shard_map/scatter-add | solution.py:62
  37.1 35.3 %all-reduce.2.cloned.1.call-done = f32[20,1024]{1,0:T(8,128)} async-done(((f32[20,1024]{1,0:T(8,128)}), f32[20,1024]{1,0:T(8,128)}) %all-reduce.2.cloned.1.call-update) | async-done | bytes 81936 | tf_op jit(solution)/shard_map/psum | solution.py:101
  75.5 14.1 %gather_fusion = f32[4096,5]{1,0:T(8,128)} fusion(f32[5,1024]{0,1:T(8,128)S(1)} %copy.273, s32[4096]{0:T(1024)S(1)} %get-tuple-element.170), kind=kCustom, calls=%fused_computation.clone | custom fusion | bytes 180224 | tf_op jit(solution)/shard_map/jit(_take)/gather | solution.py:82
  92.0 25.3 %scatter_custom_fusion.1 = f32[4,2051]{0,1:T(8,128)S(1)} fusion(s32[4096]{0:T(1024)} %get-tuple-element.166, f32[4096]{0:T(1024)S(1)} %get-tuple-element.157, f32[]{:T(128)} %constant.111.clone.1, f32[4,4096]{0,1:T(8,128)S(1)} %copy.270, f32[4096]{0:T(1024)S(1)} %fusion.83), kind=kCustom, calls=%fused_computation.77 | custom fusion | flops 49152 | bytes 131632 | tf_op jit(solution)/shard_map/scatter-add | solution.py:76
  117.3 25.4 %scatter_custom_fusion.2 = f32[4,2051]{0,1:T(8,128)S(1)} fusion(f32[4,2051]{0,1:T(8,128)S(1)} %scatter_custom_fusion.1, s32[4096]{0:T(1024)} %get-tuple-element.164, f32[4096]{0:T(1024)S(1)} %get-tuple-element.156, f32[4,4096]{0,1:T(8,128)S(1)} %copy.270, f32[4096]{0:T(1024)S(1)} %fusion.83), kind=kCustom, calls=%fused_computation.75 | custom fusion | flops 49152 | bytes 2162736 | tf_op jit(solution)/shard_map/scatter-add | solution.py:76
  142.6 25.4 %scatter_custom_fusion.3 = f32[4,2051]{0,1:T(8,128)S(1)} fusion(f32[4,2051]{0,1:T(8,128)S(1)} %scatter_custom_fusion.2, s32[4096]{0:T(1024)} %get-tuple-element.165, f32[4096]{0:T(1024)S(1)} %get-tuple-element.155, f32[4,4096]{0,1:T(8,128)S(1)} %copy.270, f32[4096]{0:T(1024)S(1)} %fusion.83), kind=kCustom, calls=%fused_computation.73 | custom fusion | flops 49152 | bytes 2162736 | tf_op jit(solution)/shard_map/scatter-add | solution.py:76
  168.1 25.4 %scatter_custom_fusion.4 = f32[4,2051]{0,1:T(8,128)S(1)} fusion(f32[4,2051]{0,1:T(8,128)S(1)} %scatter_custom_fusion.3, s32[4096]{0:T(1024)S(1)} %get-tuple-element.169, f32[4096]{0:T(1024)S(1)} %get-tuple-element.104, f32[4,4096]{0,1:T(8,128)S(1)} %copy.270, f32[4096]{0:T(1024)S(1)} %fusion.83), kind=kCustom, calls=%fused_computation.71 | custom fusion | flops 49152 | bytes 2162736 | tf_op jit(solution)/shard_map/scatter-add | solution.py:76
  201.3 36.5 %reduce-scatter.10.cloned.1.call-done = f32[256,4]{1,0:T(8,128)} async-done(((f32[2048,4]{1,0:T(8,128)}), f32[256,4]{1,0:T(8,128)}) %reduce-scatter.10.cloned.1.call-update) | async-done | bytes 4112
  237.9 10.9 %all_gather.9 = f32[4,2048]{0,1:T(8,128)S(1)} all-gather(f32[4,256]{0,1:T(8,128)} %bitcast.131), channel_id=1, replica_groups=mesh['sky'=8,'tm'=4] {'sky'}, dimensions={1}, use_global_device_ids=true | all-gather | bytes 36864 | tf_op jit(solution)/shard_map/all_gather | solution.py:111
  254.3 14.1 %gather_fusion.4 = f32[4096,4]{1,0:T(8,128)} fusion(f32[4,2051]{0,1:T(8,128)S(1)} %constant_dynamic-update-slice_fusion, s32[4096]{0:T(1024)S(1)} %get-tuple-element.162), kind=kCustom, calls=%fused_computation.6.clone | custom fusion | bytes 147456 | tf_op jit(solution)/shard_map/jit(_take)/gather | solution.py:68
  268.4 14.1 %gather_fusion.3 = f32[4096,4]{1,0:T(8,128)} fusion(f32[4,2051]{0,1:T(8,128)S(1)} %constant_dynamic-update-slice_fusion, s32[4096]{0:T(1024)S(1)} %get-tuple-element.167), kind=kCustom, calls=%fused_computation.5.clone | custom fusion | bytes 147456 | tf_op jit(solution)/shard_map/jit(_take)/gather | solution.py:68
  282.5 14.1 %gather_fusion.2 = f32[4096,4]{1,0:T(8,128)} fusion(f32[4,2051]{0,1:T(8,128)S(1)} %constant_dynamic-update-slice_fusion, s32[4096]{0:T(1024)S(1)} %get-tuple-element.168), kind=kCustom, calls=%fused_computation.4.clone | custom fusion | bytes 147456 | tf_op jit(solution)/shard_map/jit(_take)/gather | solution.py:68
  296.5 14.1 %gather_fusion.1 = f32[4096,4]{1,0:T(8,128)} fusion(f32[4,2051]{0,1:T(8,128)S(1)} %constant_dynamic-update-slice_fusion, s32[4096]{0:T(1024)S(1)} %get-tuple-element.163), kind=kCustom, calls=%fused_computation.1.clone | custom fusion | bytes 147456 | tf_op jit(solution)/shard_map/jit(_take)/gather | solution.py:68
  321.7 22.8 %scatter_custom_fusion.5 = f32[5,1024]{0,1:T(8,128)S(1)} fusion(s32[4096]{0:T(1024)} %copy-done.35, f32[4096,5]{1,0:T(8,128)} %copy.277, f32[]{:T(128)} %constant.111.clone.1), kind=kCustom, calls=%fused_computation.111 | custom fusion | flops 20480 | bytes 20992 | tf_op jit(solution)/shard_map/scatter-add | solution.py:62
  344.6 17.2 %psum.73 = f32[5,1024]{1,0:T(8,128)S(1)} all-reduce(f32[5,1024]{1,0:T(8,128)S(1)} %copy.278), channel_id=1, replica_groups=mesh['sky'=8,'tm'=4] {'tm'}, use_global_device_ids=true, to_apply=%region_17.20 | all-reduce | flops 5120 | bytes 40960 | tf_op jit(solution)/shard_map/psum | solution.py:108
  363.1 14.1 %gather_fusion.5 = f32[4096,5]{1,0:T(8,128)} fusion(f32[5,1024]{0,1:T(8,128)S(1)} %copy.279, s32[4096]{0:T(1024)S(1)} %get-tuple-element.170), kind=kCustom, calls=%fused_computation.2.clone | custom fusion | bytes 180224 | tf_op jit(solution)/shard_map/jit(_take)/gather | solution.py:82
  379.6 25.3 %scatter_custom_fusion.6 = f32[4,2051]{0,1:T(8,128)S(1)} fusion(s32[4096]{0:T(1024)} %get-tuple-element.166, f32[4096]{0:T(1024)S(1)} %get-tuple-element.154, f32[]{:T(128)} %constant.111.clone.1, f32[4,4096]{0,1:T(8,128)S(1)} %copy.270, f32[4096]{0:T(1024)S(1)} %fusion.83), kind=kCustom, calls=%fused_computation.61 | custom fusion | flops 49152 | bytes 131632 | tf_op jit(solution)/shard_map/scatter-add | solution.py:76
  404.8 25.6 %scatter_custom_fusion.7 = f32[4,2051]{0,1:T(8,128)S(1)} fusion(f32[4,2051]{0,1:T(8,128)S(1)} %scatter_custom_fusion.6, s32[4096]{0:T(1024)} %get-tuple-element.164, f32[4096]{0:T(1024)S(1)} %get-tuple-element.153, f32[4,4096]{0,1:T(8,128)S(1)} %copy.270, f32[4096]{0:T(1024)S(1)} %fusion.83), kind=kCustom, calls=%fused_computation.59 | custom fusion | flops 49152 | bytes 2162736 | tf_op jit(solution)/shard_map/scatter-add | solution.py:76
  430.5 25.4 %scatter_custom_fusion.8 = f32[4,2051]{0,1:T(8,128)S(1)} fusion(f32[4,2051]{0,1:T(8,128)S(1)} %scatter_custom_fusion.7, s32[4096]{0:T(1024)} %get-tuple-element.165, f32[4096]{0:T(1024)S(1)} %get-tuple-element.152, f32[4,4096]{0,1:T(8,128)S(1)} %copy.270, f32[4096]{0:T(1024)S(1)} %fusion.83), kind=kCustom, calls=%fused_computation.57 | custom fusion | flops 49152 | bytes 2162736 | tf_op jit(solution)/shard_map/scatter-add | solution.py:76
  455.8 25.4 %scatter_custom_fusion.9 = f32[4,2051]{0,1:T(8,128)S(1)} fusion(f32[4,2051]{0,1:T(8,128)S(1)} %scatter_custom_fusion.8, s32[4096]{0:T(1024)} %copy-done.36, f32[4096]{0:T(1024)S(1)} %get-tuple-element.93, f32[4,4096]{0,1:T(8,128)S(1)} %copy.270, f32[4096]{0:T(1024)S(1)} %fusion.83), kind=kCustom, calls=%fused_computation.55 | custom fusion | flops 49152 | bytes 2162736 | tf_op jit(solution)/shard_map/scatter-add | solution.py:76
  487.6 36.2 %reduce-scatter.12.cloned.1.call-done = f32[256,4]{1,0:T(8,128)} async-done(((f32[2048,4]{1,0:T(8,128)}), f32[256,4]{1,0:T(8,128)}) %reduce-scatter.12.cloned.1.call-update) | async-done | bytes 4112
  525.4 12.9 %psum.71 = f32[]{:T(128)} all-reduce(f32[]{:T(128)} %get-tuple-element.72), channel_id=1, replica_groups=mesh['sky'=8,'tm'=4] {'sky'}, use_global_device_ids=true, to_apply=%region_10.12 | all-reduce | flops 1 | bytes 8 | tf_op jit(solution)/shard_map/psum | solution.py:123
  538.3 12.3 %psum.72 = f32[]{:T(128)} all-reduce(f32[]{:T(128)} %psum.71), channel_id=1, replica_groups=mesh['sky'=8,'tm'=4] {'tm'}, use_global_device_ids=true, to_apply=%region_11.13 | all-reduce | flops 1 | bytes 8 | tf_op jit(solution)/shard_map/psum | solution.py:123
  550.6 37.0 %psum.74 = f32[]{:T(128)} all-reduce(f32[]{:T(128)} %get-tuple-element.71), channel_id=1, replica_groups=mesh['sky'=8,'tm'=4] {'sky','tm'}, use_global_device_ids=true, to_apply=%region_25.28 | all-reduce | flops 1 | bytes 8 | tf_op jit(solution)/shard_map/psum | solution.py:134
  589.5 13.5 %psum.75 = f32[]{:T(128)} all-reduce(f32[]{:T(128)} %multiply_reduce_fusion.1), channel_id=1, replica_groups=mesh['sky'=8,'tm'=4] {'sky'}, use_global_device_ids=true, to_apply=%region_27.30 | all-reduce | flops 1 | bytes 8 | tf_op jit(solution)/shard_map/psum | solution.py:123
  603.0 11.8 %psum.76 = f32[]{:T(128)} all-reduce(f32[]{:T(128)} %psum.75), channel_id=1, replica_groups=mesh['sky'=8,'tm'=4] {'tm'}, use_global_device_ids=true, to_apply=%region_28.31 | all-reduce | flops 1 | bytes 8 | tf_op jit(solution)/shard_map/psum | solution.py:123
  616.1 9.1 all_gather.10
  631.1 14.1 %gather_fusion.9 = f32[4096,4]{1,0:T(8,128)} fusion(f32[4,2051]{0,1:T(8,128)S(1)} %copy.282, s32[4096]{0:T(1024)S(1)} %get-tuple-element.162), kind=kCustom, calls=%fused_computation.10.clone | custom fusion | bytes 147456 | tf_op jit(solution)/shard_map/jit(_take)/gather | solution.py:68
  645.1 14.1 %gather_fusion.8 = f32[4096,4]{1,0:T(8,128)} fusion(f32[4,2051]{0,1:T(8,128)S(1)} %copy.282, s32[4096]{0:T(1024)S(1)} %get-tuple-element.167), kind=kCustom, calls=%fused_computation.9.clone | custom fusion | bytes 147456 | tf_op jit(solution)/shard_map/jit(_take)/gather | solution.py:68
  659.2 14.1 %gather_fusion.7 = f32[4096,4]{1,0:T(8,128)} fusion(f32[4,2051]{0,1:T(8,128)S(1)} %copy.282, s32[4096]{0:T(1024)S(1)} %get-tuple-element.168), kind=kCustom, calls=%fused_computation.8.clone | custom fusion | bytes 147456 | tf_op jit(solution)/shard_map/jit(_take)/gather | solution.py:68
  673.3 14.1 %gather_fusion.6 = f32[4096,4]{1,0:T(8,128)} fusion(f32[4,2051]{0,1:T(8,128)S(1)} %copy.282, s32[4096]{0:T(1024)S(1)} %get-tuple-element.163), kind=kCustom, calls=%fused_computation.7.clone | custom fusion | bytes 147456 | tf_op jit(solution)/shard_map/jit(_take)/gather | solution.py:68
  687.4 9.5 fusion.15
  699.0 22.8 %scatter_custom_fusion.10 = f32[5,1024]{0,1:T(8,128)S(1)} fusion(s32[4096]{0:T(1024)} %copy-done.35, f32[4096,5]{1,0:T(8,128)} %copy.286, f32[]{:T(128)} %constant.111.clone.1), kind=kCustom, calls=%fused_computation.109 | custom fusion | flops 20480 | bytes 20992 | tf_op jit(solution)/shard_map/scatter-add | solution.py:62
  722.0 15.8 %psum.77 = f32[5,1024]{1,0:T(8,128)S(1)} all-reduce(f32[5,1024]{1,0:T(8,128)S(1)} %copy.287), channel_id=1, replica_groups=mesh['sky'=8,'tm'=4] {'tm'}, use_global_device_ids=true, to_apply=%region_34.37 | all-reduce | flops 5120 | bytes 40960 | tf_op jit(solution)/shard_map/psum | solution.py:108
  739.1 14.1 %gather_fusion.10 = f32[4096,5]{1,0:T(8,128)} fusion(f32[5,1024]{0,1:T(8,128)S(1)} %copy.288, s32[4096]{0:T(1024)S(1)} %get-tuple-element.170), kind=kCustom, calls=%fused_computation.3.clone | custom fusion | bytes 180224 | tf_op jit(solution)/shard_map/jit(_take)/gather | solution.py:82
  755.5 25.3 %scatter_custom_fusion.11 = f32[4,2051]{0,1:T(8,128)S(1)} fusion(s32[4096]{0:T(1024)} %get-tuple-element.166, f32[4096]{0:T(1024)S(1)} %get-tuple-element.151, f32[]{:T(128)} %constant.111.clone.1, f32[4,4096]{0,1:T(8,128)S(1)} %copy.270, f32[4096]{0:T(1024)S(1)} %fusion.83), kind=kCustom, calls=%fused_computation.45 | custom fusion | flops 49152 | bytes 131632 | tf_op jit(solution)/shard_map/scatter-add | solution.py:76
  780.8 25.4 %scatter_custom_fusion.12 = f32[4,2051]{0,1:T(8,128)S(1)} fusion(f32[4,2051]{0,1:T(8,128)S(1)} %scatter_custom_fusion.11, s32[4096]{0:T(1024)} %get-tuple-element.164, f32[4096]{0:T(1024)S(1)} %get-tuple-element.150, f32[4,4096]{0,1:T(8,128)S(1)} %copy.270, f32[4096]{0:T(1024)S(1)} %fusion.83), kind=kCustom, calls=%fused_computation.43 | custom fusion | flops 49152 | bytes 2162736 | tf_op jit(solution)/shard_map/scatter-add | solution.py:76
  806.2 25.4 %scatter_custom_fusion.13 = f32[4,2051]{0,1:T(8,128)S(1)} fusion(f32[4,2051]{0,1:T(8,128)S(1)} %scatter_custom_fusion.12, s32[4096]{0:T(1024)} %get-tuple-element.165, f32[4096]{0:T(1024)S(1)} %get-tuple-element.149, f32[4,4096]{0,1:T(8,128)S(1)} %copy.270, f32[4096]{0:T(1024)S(1)} %fusion.83), kind=kCustom, calls=%fused_computation.41 | custom fusion | flops 49152 | bytes 2162736 | tf_op jit(solution)/shard_map/scatter-add | solution.py:76
  831.6 25.6 %scatter_custom_fusion.14 = f32[4,2051]{0,1:T(8,128)S(1)} fusion(f32[4,2051]{0,1:T(8,128)S(1)} %scatter_custom_fusion.13, s32[4096]{0:T(1024)} %copy-done.36, f32[4096]{0:T(1024)S(1)} %get-tuple-element.82, f32[4,4096]{0,1:T(8,128)S(1)} %copy.270, f32[4096]{0:T(1024)S(1)} %fusion.83), kind=kCustom, calls=%fused_computation.39 | custom fusion | flops 49152 | bytes 2162736 | tf_op jit(solution)/shard_map/scatter-add | solution.py:76
  863.4 36.8 %reduce-scatter.14.cloned.1.call-done = f32[256,4]{1,0:T(8,128)} async-done(((f32[2048,4]{1,0:T(8,128)}), f32[256,4]{1,0:T(8,128)}) %reduce-scatter.14.cloned.1.call-update) | async-done | bytes 4112
  901.8 39.5 %psum.78 = f32[]{:T(128)} all-reduce(f32[]{:T(128)} %multiply_reduce_fusion), channel_id=1, replica_groups=mesh['sky'=8,'tm'=4] {'sky','tm'}, use_global_device_ids=true, to_apply=%region_42.45 | all-reduce | flops 1 | bytes 8 | tf_op jit(solution)/shard_map/psum | solution.py:134
  943.3 10.1 all_gather.11
  959.8 14.1 %gather_fusion.14 = f32[4096,4]{1,0:T(8,128)} fusion(f32[4,2051]{0,1:T(8,128)S(1)} %copy.291, s32[4096]{0:T(1024)S(1)} %get-tuple-element.162), kind=kCustom, calls=%fused_computation.14.clone | custom fusion | bytes 147456 | tf_op jit(solution)/shard_map/jit(_take)/gather | solution.py:68
  973.8 14.1 %gather_fusion.13 = f32[4096,4]{1,0:T(8,128)} fusion(f32[4,2051]{0,1:T(8,128)S(1)} %copy.291, s32[4096]{0:T(1024)S(1)} %get-tuple-element.167), kind=kCustom, calls=%fused_computation.13.clone | custom fusion | bytes 147456 | tf_op jit(solution)/shard_map/jit(_take)/gather | solution.py:68
  987.9 14.1 %gather_fusion.12 = f32[4096,4]{1,0:T(8,128)} fusion(f32[4,2051]{0,1:T(8,128)S(1)} %copy.291, s32[4096]{0:T(1024)S(1)} %get-tuple-element.168), kind=kCustom, calls=%fused_computation.12.clone | custom fusion | bytes 147456 | tf_op jit(solution)/shard_map/jit(_take)/gather | solution.py:68
  1002.0 14.1 %gather_fusion.11 = f32[4096,4]{1,0:T(8,128)} fusion(f32[4,2051]{0,1:T(8,128)S(1)} %copy.291, s32[4096]{0:T(1024)S(1)} %get-tuple-element.163), kind=kCustom, calls=%fused_computation.11.clone | custom fusion | bytes 147456 | tf_op jit(solution)/shard_map/jit(_take)/gather | solution.py:68
  1025.8 22.6 %scatter_custom_fusion.15 = f32[5,1024]{0,1:T(8,128)S(1)} fusion(s32[4096]{0:T(1024)} %copy-done.35, f32[4096,5]{1,0:T(8,128)S(1)} %copy.295, f32[]{:T(128)} %constant.111.clone.1), kind=kCustom, calls=%fused_computation.107 | custom fusion | flops 20480 | bytes 20992 | tf_op jit(solution)/shard_map/scatter-add | solution.py:62
  1048.6 17.1 %psum.79 = f32[5,1024]{1,0:T(8,128)S(1)} all-reduce(f32[5,1024]{1,0:T(8,128)S(1)} %copy.296), channel_id=1, replica_groups=mesh['sky'=8,'tm'=4] {'tm'}, use_global_device_ids=true, to_apply=%region_48.51 | all-reduce | flops 5120 | bytes 40960 | tf_op jit(solution)/shard_map/psum | solution.py:108
  (180 shorter events, 86.5 us)
Async XLA Ops:
  7.2 65.2 %all-reduce.2.cloned.1.call-start = ((), (), s32[]{:S(2)}) async-start(), calls=%async_computation.3 | async-start | bytes 196608 | tf_op jit(solution)/shard_map/psum | solution.py:101
  9.8 25.2 %copy-start.35 = (s32[4096]{0:T(1024)}, s32[4096]{0:T(1024)S(1)}, u32[]{:S(2)}) copy-start(s32[4096]{0:T(1024)S(1)} %get-tuple-element.171) | copy-start | bytes 49156
  10.5 24.6 %copy-start.25 = (s32[4096]{0:T(1024)S(1)}, s32[4096]{0:T(1024)}, u32[]{:S(2)}) copy-start(s32[4096]{0:T(1024)} %param.19) | copy-start | bytes 49156
  11.0 24.7 %copy-start.24 = (s32[4096]{0:T(1024)S(1)}, s32[4096]{0:T(1024)}, u32[]{:S(2)}) copy-start(s32[4096]{0:T(1024)} %param.18) | copy-start | bytes 49156
  11.0 24.7 %copy-start.23 = (f32[4,4096]{1,0:T(4,128)S(1)}, f32[4,4096]{1,0:T(4,128)}, u32[]{:S(2)}) copy-start(f32[4,4096]{1,0:T(4,128)} %param.22) | copy-start | bytes 196612
  11.7 60.7 %copy-start.34 = (f32[5,1024]{1,0:T(8,128)S(1)}, f32[5,1024]{1,0:T(8,128)}, u32[]{:S(2)}) copy-start(f32[5,1024]{1,0:T(8,128)} %param.25) | copy-start | bytes 61444
  35.0 202.8 %reduce-scatter.10.cloned.1.call-start = ((), (), s32[]{:S(2)}) async-start(), calls=%async_computation.4 | async-start | bytes 1179648
  35.7 132.3 %copy-start.36 = (s32[4096]{0:T(1024)}, s32[4096]{0:T(1024)S(1)}, u32[]{:S(2)}) copy-start(s32[4096]{0:T(1024)S(1)} %get-tuple-element.169) | copy-start | bytes 49156
  35.7 343.7 %copy-start.21 = (pred[4096]{0:T(1024)(128)(4,1)}, pred[4096]{0:T(1024)(128)(4,1)S(1)}, u32[]{:S(2)}) copy-start(pred[4096]{0:T(1024)(128)(4,1)S(1)} %compare_and_fusion.4) | copy-start | bytes 12292
  73.6 288.4 %copy-start.3 = (f32[1,1024]{1,0:T(1,128)}, f32[1,1024]{1,0:T(1,128)S(1)}, u32[]{:S(2)}) copy-start(f32[1,1024]{1,0:T(1,128)S(1)} %get-tuple-element.126) | copy-start | bytes 12292
  73.6 288.4 %copy-start.5 = (f32[1,1024]{1,0:T(1,128)}, f32[1,1024]{1,0:T(1,128)S(1)}, u32[]{:S(2)}) copy-start(f32[1,1024]{1,0:T(1,128)S(1)} %get-tuple-element.127) | copy-start | bytes 12292
  73.6 288.4 %copy-start.7 = (f32[1,1024]{1,0:T(1,128)}, f32[1,1024]{1,0:T(1,128)S(1)}, u32[]{:S(2)}) copy-start(f32[1,1024]{1,0:T(1,128)S(1)} %get-tuple-element.128) | copy-start | bytes 12292
  73.6 18.2 %copy-start = (f32[5,4096]{1,0:T(8,128)S(1)}, f32[5,4096]{1,0:T(8,128)}, u32[]{:S(2)}) copy-start(f32[5,4096]{1,0:T(8,128)} %param.21) | copy-start | bytes 245764
  75.3 16.6 %copy-start.1 = (f32[4096]{0:T(1024)S(1)}, f32[4096]{0:T(1024)}, u32[]{:S(2)}) copy-start(f32[4096]{0:T(1024)} %param.23) | copy-start | bytes 49156
  75.3 16.6 %copy-start.9 = (f32[4096]{0:T(1024)S(1)}, f32[4096]{0:T(1024)}, u32[]{:S(2)}) copy-start(f32[4096]{0:T(1024)} %param.24) | copy-start | bytes 49156
  194.6 4.6 collective-permute-start
  201.2 322.6 %reduce-scatter.12.cloned.1.call-start = ((), (), s32[]{:S(2)}) async-start(), calls=%async_computation.5 | async-start | bytes 1179648
  201.3 109.3 %copy-start.13 = (pred[4096]{0:T(1024)(128)(4,1)}, pred[4096]{0:T(1024)(128)(4,1)S(1)}, u32[]{:S(2)}) copy-start(pred[4096]{0:T(1024)(128)(4,1)S(1)} %get-tuple-element.158) | copy-start | bytes 12292
  201.3 109.3 %copy-start.15 = (pred[4096]{0:T(1024)(128)(4,1)}, pred[4096]{0:T(1024)(128)(4,1)S(1)}, u32[]{:S(2)}) copy-start(pred[4096]{0:T(1024)(128)(4,1)S(1)} %get-tuple-element.159) | copy-start | bytes 12292
  201.3 109.3 %copy-start.17 = (pred[4096]{0:T(1024)(128)(4,1)}, pred[4096]{0:T(1024)(128)(4,1)S(1)}, u32[]{:S(2)}) copy-start(pred[4096]{0:T(1024)(128)(4,1)S(1)} %get-tuple-element.160) | copy-start | bytes 12292
  201.3 109.3 %copy-start.19 = (pred[4096]{0:T(1024)(128)(4,1)}, pred[4096]{0:T(1024)(128)(4,1)S(1)}, u32[]{:S(2)}) copy-start(pred[4096]{0:T(1024)(128)(4,1)S(1)} %get-tuple-element.161) | copy-start | bytes 12292
  248.8 5.5 collective-permute-start.1
  319.6 42.4 %copy-start.26 = (f32[1,1024]{1,0:T(1,128)S(1)}, f32[1,1024]{1,0:T(1,128)}, u32[]{:S(2)}) copy-start(f32[1,1024]{1,0:T(1,128)} %get-tuple-element.111) | copy-start | bytes 12292
  319.6 42.4 %copy-start.28 = (f32[1,1024]{1,0:T(1,128)S(1)}, f32[1,1024]{1,0:T(1,128)}, u32[]{:S(2)}) copy-start(f32[1,1024]{1,0:T(1,128)} %get-tuple-element.112) | copy-start | bytes 12292
  319.6 42.4 %copy-start.30 = (f32[1,1024]{1,0:T(1,128)S(1)}, f32[1,1024]{1,0:T(1,128)}, u32[]{:S(2)}) copy-start(f32[1,1024]{1,0:T(1,128)} %get-tuple-element.113) | copy-start | bytes 12292
  319.6 42.4 %copy-start.32 = (f32[1,1024]{1,0:T(1,128)S(1)}, f32[1,1024]{1,0:T(1,128)}, u32[]{:S(2)}) copy-start(f32[1,1024]{1,0:T(1,128)} %get-tuple-element.114) | copy-start | bytes 12292
  481.2 6.3 copy-start.2
  482.3 2.6 collective-permute-start.2
  487.5 412.7 %reduce-scatter.14.cloned.1.call-start = ((), (), s32[]{:S(2)}) async-start(), calls=%async_computation.6 | async-start | bytes 1179648
  487.6 143.0 %copy-start.11 = (f32[4,256]{1,0:T(4,128)}, f32[4,256]{1,0:T(4,128)S(1)}, u32[]{:S(2)}) copy-start(f32[4,256]{1,0:T(4,128)S(1)} %copy.300) | copy-start | bytes 12292
  625.2 5.5 collective-permute-start.3
  696.9 40.9 %copy-start.4 = (f32[1,1024]{1,0:T(1,128)S(1)}, f32[1,1024]{1,0:T(1,128)}, u32[]{:S(2)}) copy-start(f32[1,1024]{1,0:T(1,128)} %copy-done.3) | copy-start | bytes 12292
  696.9 40.9 %copy-start.6 = (f32[1,1024]{1,0:T(1,128)S(1)}, f32[1,1024]{1,0:T(1,128)}, u32[]{:S(2)}) copy-start(f32[1,1024]{1,0:T(1,128)} %copy-done.5) | copy-start | bytes 12292
  696.9 40.9 %copy-start.8 = (f32[1,1024]{1,0:T(1,128)S(1)}, f32[1,1024]{1,0:T(1,128)}, u32[]{:S(2)}) copy-start(f32[1,1024]{1,0:T(1,128)} %copy-done.7) | copy-start | bytes 12292
  696.9 41.0 %copy-start.27 = (f32[1,1024]{1,0:T(1,128)S(1)}, f32[1,1024]{1,0:T(1,128)}, u32[]{:S(2)}) copy-start(f32[1,1024]{1,0:T(1,128)} %get-tuple-element.111) | copy-start | bytes 12292
  696.9 41.0 %copy-start.29 = (f32[1,1024]{1,0:T(1,128)S(1)}, f32[1,1024]{1,0:T(1,128)}, u32[]{:S(2)}) copy-start(f32[1,1024]{1,0:T(1,128)} %get-tuple-element.112) | copy-start | bytes 12292
  696.9 41.0 %copy-start.31 = (f32[1,1024]{1,0:T(1,128)S(1)}, f32[1,1024]{1,0:T(1,128)}, u32[]{:S(2)}) copy-start(f32[1,1024]{1,0:T(1,128)} %get-tuple-element.113) | copy-start | bytes 12292
  697.0 41.0 %copy-start.33 = (f32[1,1024]{1,0:T(1,128)S(1)}, f32[1,1024]{1,0:T(1,128)}, u32[]{:S(2)}) copy-start(f32[1,1024]{1,0:T(1,128)} %get-tuple-element.114) | copy-start | bytes 12292
  737.9 17.5 %copy-start.22 = (pred[4096]{0:T(1024)(128)(4,1)S(1)}, pred[4096]{0:T(1024)(128)(4,1)}, u32[]{:S(2)}) copy-start(pred[4096]{0:T(1024)(128)(4,1)} %copy-done.21) | copy-start | bytes 12292
  857.2 85.5 %copy-start.12 = (f32[4,256]{1,0:T(4,128)S(1)}, f32[4,256]{1,0:T(4,128)}, u32[]{:S(2)}) copy-start(f32[4,256]{1,0:T(4,128)} %copy-done.11) | copy-start | bytes 12292
  858.2 3.2 collective-permute-start.4
  863.4 152.7 %copy-start.14 = (pred[4096]{0:T(1024)(128)(4,1)S(1)}, pred[4096]{0:T(1024)(128)(4,1)}, u32[]{:S(2)}) copy-start(pred[4096]{0:T(1024)(128)(4,1)} %copy-done.13) | copy-start | bytes 12292
  863.4 152.7 %copy-start.16 = (pred[4096]{0:T(1024)(128)(4,1)S(1)}, pred[4096]{0:T(1024)(128)(4,1)}, u32[]{:S(2)}) copy-start(pred[4096]{0:T(1024)(128)(4,1)} %copy-done.15) | copy-start | bytes 12292
  863.4 152.7 %copy-start.18 = (pred[4096]{0:T(1024)(128)(4,1)S(1)}, pred[4096]{0:T(1024)(128)(4,1)}, u32[]{:S(2)}) copy-start(pred[4096]{0:T(1024)(128)(4,1)} %copy-done.17) | copy-start | bytes 12292
  863.4 152.7 %copy-start.20 = (pred[4096]{0:T(1024)(128)(4,1)S(1)}, pred[4096]{0:T(1024)(128)(4,1)}, u32[]{:S(2)}) copy-start(pred[4096]{0:T(1024)(128)(4,1)} %copy-done.19) | copy-start | bytes 12292
  953.9 5.5 collective-permute-start.5
  1016.1 9.0 copy-start.10
Sparse Core Ops, SparseCore 0:
  35.1 37.1 all-reduce.1
  201.3 36.4 reduce-scatter.9
  487.6 36.1 reduce-scatter.11
  863.5 36.6 reduce-scatter.13
